TPU v7x, 128 devices: a whole 4x4x4 slice. The times are simulated.
128 devices in a mesh: band: 8 (over x, core), grid: 16 (over z, y).
Axes of the slice: x: 4, y: 4, z: 4, core: 2. Of those that a mesh axis runs over, the one named last changes fastest.
Arguments:
- orbitals: bfloat16 [32768, 2048], P('grid', 'band'), may hold values from -6 to 6
- projectors: bfloat16 [128, 8, 128], replicated, may hold values from -0.5 to 0.5
- sphere_start: int32 [128], replicated, may hold values from 0 to 1920, as said below
- proj_count: int32 [128], replicated, may hold values from 1 to 8
- owner_slab: int32 [128], replicated, may hold values from 0 to 15, as said below
- correlation_coef: float32 [128, 8, 8], replicated, as said below
Outputs:
- rotated: bfloat16 [32768, 2048], P(('grid', 'band'))
Inputs may be any that keep to these rules, and one draw needn't show every extreme that they name: `sphere_start`: a multiple of 128. `owner_slab`: every slab owns exactly 8 atoms. `correlation_coef`: each atom's matrix is symmetric positive definite.
All inputs are finite; a program needn't handle non-finite values.
Results may differ from a plain program's by a relative error of at most 0.0049.
Values may be sent and summed in bfloat16 or wider, within the bound.
A program may use at most 128 MiB of HBM per device.

v0:
```python
import jax
import jax.numpy as jnp
from jax import lax
from jax.sharding import PartitionSpec as P

SPH = 128
NPMAX = 8
A_SLAB = 8


def inverse_factor(matrix):
    order = matrix.shape[0]
    if order <= 512 or order % 2 != 0:
        lower = jnp.linalg.cholesky(matrix)
        identity = jnp.eye(order, dtype=matrix.dtype)
        return lax.linalg.triangular_solve(lower, identity, left_side=True, lower=True)
    half = order // 2
    upper_inv = inverse_factor(matrix[:half, :half])
    below = jnp.dot(matrix[half:, :half], upper_inv.T, precision=lax.Precision.HIGHEST)
    schur = matrix[half:, half:] - jnp.dot(below, below.T, precision=lax.Precision.HIGHEST)
    lower_inv = inverse_factor(schur)
    corner = -jnp.dot(
        lower_inv,
        jnp.dot(below, upper_inv, precision=lax.Precision.HIGHEST),
        precision=lax.Precision.HIGHEST,
    )
    top = jnp.concatenate([upper_inv, jnp.zeros((half, order - half), matrix.dtype)], axis=1)
    bottom = jnp.concatenate([corner, lower_inv], axis=1)
    return jnp.concatenate([top, bottom], axis=0)


def slab_atoms(owner_slab, slab):
    atoms = owner_slab.shape[0]
    keyed = jnp.where(owner_slab == slab, 0, 1) * atoms + jnp.arange(atoms, dtype=jnp.int32)
    return jnp.argsort(keyed, stable=True)[:A_SLAB]


def atom_terms(source, weights, starts, counts, coefs, valid):

    def take_rows(offset):
        return lax.dynamic_slice_in_dim(source, offset, SPH, 0)

    sphere_rows = jax.vmap(take_rows)(starts)
    correlations = jnp.einsum(
        "aij,ajn->ain", weights, sphere_rows, preferred_element_type=jnp.float32
    )
    active = (jnp.arange(NPMAX)[None, :] < counts[:, None]) & valid[:, None]
    correlations = jnp.where(active[:, :, None], correlations, jnp.zeros_like(correlations))
    weighted = jnp.einsum("aij,ajn->ain", coefs, correlations, precision=lax.Precision.HIGHEST)
    return (correlations, weighted)


def shards(orbitals, projectors, sphere_start, proj_count, owner_slab, correlation_coef):
    band_index = lax.axis_index("band")
    slab = lax.axis_index("grid")
    nbands = lax.axis_size("band")
    total_rows = orbitals.shape[0] * lax.axis_size("grid")
    chosen = slab_atoms(owner_slab, slab)
    weights = projectors[chosen]
    counts = proj_count[chosen]
    coefs = correlation_coef[chosen]
    gathered = lax.all_gather(orbitals, "band", axis=1, tiled=True)
    width = orbitals.shape[1]
    width_all = gathered.shape[1]
    gram_panel = jnp.dot(orbitals.T, gathered, preferred_element_type=jnp.float32) * (
        1.0 / total_rows
    )
    valid = jnp.ones((A_SLAB,), dtype=bool)
    correlations, weighted = atom_terms(
        gathered, weights, sphere_start[chosen], counts, coefs, valid
    )
    panel_weighted = lax.dynamic_slice_in_dim(weighted, band_index * width, width, 2)
    paw = jnp.dot(
        panel_weighted.reshape(-1, width).T,
        correlations.reshape(-1, width_all),
        precision=lax.Precision.HIGHEST,
    )
    panel_total = lax.psum(gram_panel + paw, "grid")
    metric = lax.all_gather(panel_total, "band", axis=0, tiled=True)
    height = orbitals.shape[0] // nbands
    mine = lax.dynamic_slice_in_dim(gathered, band_index * height, height, 0)
    inverse = inverse_factor(metric).astype(jnp.bfloat16)
    return jnp.dot(mine, inverse.T, preferred_element_type=jnp.float32).astype(jnp.bfloat16)


def solution(mesh):
    in_specs = (P("grid", "band"), P(), P(), P(), P(), P())
    out_specs = P(("grid", "band"), None)
    return jax.shard_map(shards, mesh=mesh, in_specs=in_specs, out_specs=out_specs, check_vma=False)
```

profile of v0, /device:TPU:1, one launch (start us, length us, event | category | flops | bytes accessed | tf_op | source)
XLA Modules:
  0.0 1023.9 jit_solution(12298596556159580187)
XLA Ops:
  15.4 50.7 %all-gather.3.cloned.1.call-done = bf16[2048,2048]{1,0:T(8,128)(2,1)} async-done(((bf16[2048,256]{1,0:T(8,128)(2,1)}), bf16[2048,2048]{1,0:T(8,128)(2,1)}) %all-gather.3.cloned.1.call-update) | async-done | bytes 8388624 | tf_op jit(solution)/shard_map/all_gather | solution.py:62
  66.1 25.7 %while.9 = (s32[]{:T(128)}, bf16[2048,2048]{1,0:T(8,128)(2,1)}, s32[8,2]{0,1:T(2,128)S(1)}, bf16[8,128,2048]{2,1,0:T(8,128)(2,1)}, s32[]{:T(128)}) while((s32[]{:T(128)}, bf16[2048,2048]{1,0:T(8,128)(2,1)}, s32[8,2]{0,1:T(2,128)S(1)}, bf16[8,128,2048]{2,1,0:T(8,128)(2,1)}, s32[]{:T(128)}) %tuple.104), condition=%wide.while_cond.1, body=%wide.while_body.1.sunk | while | flops 2 | bytes 1049189 | solution.py:41
  95.3 6.8 convolution_multiply_fusion
  105.5 90.3 %all-reduce.7.cloned.1.call-done = f32[256,2048]{0,1:T(8,128)} async-done(((f32[256,2048]{0,1:T(8,128)}), f32[256,2048]{0,1:T(8,128)}) %all-reduce.7.cloned.1.call-update) | async-done | bytes 2097168 | tf_op jit(solution)/shard_map/psum | solution.py:78
  196.0 87.6 %all-gather.5.cloned.1.call-done = f32[2048,2048]{0,1:T(8,128)} async-done(((f32[256,2048]{0,1:T(8,128)}), f32[2048,2048]{0,1:T(8,128)}) %all-gather.5.cloned.1.call-update) | async-done | bytes 16777232 | tf_op jit(solution)/shard_map/all_gather | solution.py:79
  286.7 11.7 %cholesky.462 = f32[128,128]{1,0:T(8,128)S(1)} custom-call(f32[128,128]{1,0:T(8,128)S(1)} %cholesky.746), custom_call_target="Cholesky" | custom-call | tf_op jit(solution)/shard_map/jit(cholesky)/cholesky | solution.py:14
  298.6 9.8 custom-call.35
  309.1 11.7 %cholesky.481 = f32[128,128]{1,0:T(8,128)S(1)} custom-call(f32[128,128]{1,0:T(8,128)S(1)} %cholesky.750), custom_call_target="Cholesky" | custom-call | tf_op jit(solution)/shard_map/jit(cholesky)/cholesky | solution.py:14
  320.8 10.3 %custom-call.36 = f32[1,128,128]{1,2,0:T(8,128)S(1)} custom-call(f32[1,128,128]{2,1,0:T(8,128)S(1)} %get-tuple-element.131), custom_call_target="InvertDiagBlocksLowerTriangular" | custom-call | tf_op jit(solution)/shard_map/jit(cholesky)/cholesky | solution.py:14
  331.8 11.7 %cholesky.502 = f32[128,128]{1,0:T(8,128)S(1)} custom-call(f32[128,128]{1,0:T(8,128)S(1)} %cholesky.755), custom_call_target="Cholesky" | custom-call | tf_op jit(solution)/shard_map/jit(cholesky)/cholesky | solution.py:14
  343.5 9.8 custom-call.37
  353.9 11.7 %cholesky.519 = f32[128,128]{1,0:T(8,128)S(1)} custom-call(f32[128,128]{1,0:T(8,128)S(1)} %convolution_subtract_fusion.25), custom_call_target="Cholesky" | custom-call | tf_op jit(solution)/shard_map/jit(cholesky)/cholesky | solution.py:14
  370.5 7.6 while.10
  378.1 39.3 %custom-call.38 = f32[4,128,128]{1,2,0:T(8,128)S(1)} custom-call(f32[4,128,128]{2,1,0:T(8,128)S(1)} %get-tuple-element.43), custom_call_target="InvertDiagBlocksLowerTriangular" | custom-call | tf_op jit(solution)/shard_map/triangular_solve/custom-call.3 | solution.py:16
  435.1 12.1 %cholesky.534 = f32[128,128]{1,0:T(8,128)S(1)} custom-call(f32[128,128]{1,0:T(8,128)S(1)} %cholesky.759), custom_call_target="Cholesky" | custom-call | tf_op jit(solution)/shard_map/jit(cholesky)/cholesky | solution.py:14
  447.4 9.8 custom-call.39
  459.7 11.7 %cholesky.553 = f32[128,128]{1,0:T(8,128)S(1)} custom-call(f32[128,128]{1,0:T(8,128)S(1)} %cholesky.763), custom_call_target="Cholesky" | custom-call | tf_op jit(solution)/shard_map/jit(cholesky)/cholesky | solution.py:14
  471.5 9.8 custom-call.40
  482.8 11.9 %cholesky.574 = f32[128,128]{1,0:T(8,128)S(1)} custom-call(f32[128,128]{1,0:T(8,128)S(1)} %cholesky.768), custom_call_target="Cholesky" | custom-call | tf_op jit(solution)/shard_map/jit(cholesky)/cholesky | solution.py:14
  494.8 9.8 custom-call.41
  506.0 11.7 %cholesky.591 = f32[128,128]{1,0:T(8,128)S(1)} custom-call(f32[128,128]{1,0:T(8,128)S(1)} %convolution_subtract_fusion.24), custom_call_target="Cholesky" | custom-call | tf_op jit(solution)/shard_map/jit(cholesky)/cholesky | solution.py:14
  523.9 11.2 %while.11 = (s32[]{:T(128)}, f32[512,512]{1,0:T(8,128)}, s32[4,2]{0,1:T(2,128)S(1)}, f32[4,128,128]{2,1,0:T(8,128)S(1)}, s32[]{:T(128)}) while((s32[]{:T(128)}, f32[512,512]{1,0:T(8,128)}, s32[4,2]{0,1:T(2,128)S(1)}, f32[4,128,128]{2,1,0:T(8,128)S(1)}, s32[]{:T(128)}) %tuple.125), condition=%wide.while_cond.clone, body=%wide.while_body.clone.sunk | while | flops 2 | bytes 131189 | solution.py:16
  535.1 39.5 %custom-call.42 = f32[4,128,128]{1,2,0:T(8,128)S(1)} custom-call(f32[4,128,128]{2,1,0:T(8,128)S(1)} %get-tuple-element.44), custom_call_target="InvertDiagBlocksLowerTriangular" | custom-call | tf_op jit(solution)/shard_map/triangular_solve/custom-call.3 | solution.py:16
  583.3 7.0 fusion.173
  590.3 28.5 %fusion.9 = f32[1024,1024]{1,0:T(8,128)S(1)} fusion(f32[2048,2048]{0,1:T(8,128)} %all-gather.5.cloned.1.call-done, f32[512,512]{1,0:T(8,128)S(1)} %copy-done.5, f32[128,512]{1,0:T(8,128)S(1)} %fusion.125, f32[128,512]{1,0:T(8,128)S(1)} %fusion.126, f32[128,512]{1,0:T(8,128)S(1)} %fusion.128, f32[128,512]{1,0:T(8,128)S(1)} %fusion.81, ...), kind=kOutput, calls=%fused_computation.24 | convolution fusion | flops 12892241920 | bytes 11534336 | tf_op jit(solution)/shard_map/dot_general | solution.py:19
  618.8 18.2 %slice_subtract_fusion = f32[1024,1024]{0,1:T(8,128)} fusion(f32[2048,2048]{0,1:T(8,128)} %all-gather.5.cloned.1.call-done, f32[1024,1024]{1,0:T(8,128)S(1)} %fusion.9), kind=kOutput, calls=%fused_computation.26 | convolution fusion | flops 12885950464 | bytes 16777216 | tf_op jit(solution)/shard_map/dot_general | solution.py:20
  643.3 11.7 %cholesky.606 = f32[128,128]{1,0:T(8,128)S(1)} custom-call(f32[128,128]{1,0:T(8,128)S(1)} %cholesky.772), custom_call_target="Cholesky" | custom-call | tf_op jit(solution)/shard_map/jit(cholesky)/cholesky | solution.py:14
  655.2 9.8 custom-call.43
  667.5 11.7 %cholesky.625 = f32[128,128]{1,0:T(8,128)S(1)} custom-call(f32[128,128]{1,0:T(8,128)S(1)} %cholesky.776), custom_call_target="Cholesky" | custom-call | tf_op jit(solution)/shard_map/jit(cholesky)/cholesky | solution.py:14
  679.3 10.3 %custom-call.44 = f32[1,128,128]{1,2,0:T(8,128)S(1)} custom-call(f32[1,128,128]{2,1,0:T(8,128)S(1)} %get-tuple-element.111), custom_call_target="InvertDiagBlocksLowerTriangular" | custom-call | tf_op jit(solution)/shard_map/jit(cholesky)/cholesky | solution.py:14
  691.1 11.7 %cholesky.646 = f32[128,128]{1,0:T(8,128)S(1)} custom-call(f32[128,128]{1,0:T(8,128)S(1)} %cholesky.781), custom_call_target="Cholesky" | custom-call | tf_op jit(solution)/shard_map/jit(cholesky)/cholesky | solution.py:14
  702.9 9.8 custom-call.45
  714.1 11.7 %cholesky.663 = f32[128,128]{1,0:T(8,128)S(1)} custom-call(f32[128,128]{1,0:T(8,128)S(1)} %convolution_subtract_fusion.23), custom_call_target="Cholesky" | custom-call | tf_op jit(solution)/shard_map/jit(cholesky)/cholesky | solution.py:14
  732.4 11.7 %while.12 = (s32[]{:T(128)}, f32[512,512]{1,0:T(8,128)}, s32[4,2]{0,1:T(2,128)S(1)}, f32[4,128,128]{2,1,0:T(8,128)S(1)}, s32[]{:T(128)}) while((s32[]{:T(128)}, f32[512,512]{1,0:T(8,128)}, s32[4,2]{0,1:T(2,128)S(1)}, f32[4,128,128]{2,1,0:T(8,128)S(1)}, s32[]{:T(128)}) %tuple.126), condition=%wide.while_cond.clone.1, body=%wide.while_body.clone.1.sunk | while | flops 2 | bytes 131189 | solution.py:16
  744.1 39.3 %custom-call.46 = f32[4,128,128]{1,2,0:T(8,128)S(1)} custom-call(f32[4,128,128]{2,1,0:T(8,128)S(1)} %get-tuple-element.45), custom_call_target="InvertDiagBlocksLowerTriangular" | custom-call | tf_op jit(solution)/shard_map/triangular_solve/custom-call.3 | solution.py:16
  801.2 17.2 %fusion.172 = f32[1024,1024]{1,0:T(8,128)} fusion(f32[1024,1024]{1,0:T(8,128)S(1)} %copy-done.17, f32[512,512]{1,0:T(8,128)S(1)} %copy-done.6, f32[128,512]{1,0:T(8,128)S(1)} %copy-done.12, f32[128,512]{1,0:T(8,128)S(1)} %fusion.126, f32[128,512]{1,0:T(8,128)S(1)} %fusion.128, f32[128,512]{1,0:T(8,128)S(1)} %fusion.81, f32[512,512]{1,0:T(8,128)S(1)} %copy-done.3), kind=kOutput, calls=%fused_computation.324 | convolution fusion | flops 12892241920 | bytes 11534336 | tf_op jit(solution)/shard_map/dot_general | solution.py:24
  822.1 11.7 %cholesky.678 = f32[128,128]{1,0:T(8,128)S(1)} custom-call(f32[128,128]{1,0:T(8,128)S(1)} %cholesky.785), custom_call_target="Cholesky" | custom-call | tf_op jit(solution)/shard_map/jit(cholesky)/cholesky | solution.py:14
  834.0 9.8 custom-call.47
  846.4 11.7 %cholesky.697 = f32[128,128]{1,0:T(8,128)S(1)} custom-call(f32[128,128]{1,0:T(8,128)S(1)} %cholesky.789), custom_call_target="Cholesky" | custom-call | tf_op jit(solution)/shard_map/jit(cholesky)/cholesky | solution.py:14
  858.1 10.0 custom-call.48
  869.6 11.7 %cholesky.718 = f32[128,128]{1,0:T(8,128)S(1)} custom-call(f32[128,128]{1,0:T(8,128)S(1)} %cholesky.794), custom_call_target="Cholesky" | custom-call | tf_op jit(solution)/shard_map/jit(cholesky)/cholesky | solution.py:14
  881.4 9.8 custom-call.49
  892.6 11.7 %cholesky.735 = f32[128,128]{1,0:T(8,128)S(1)} custom-call(f32[128,128]{1,0:T(8,128)S(1)} %convolution_subtract_fusion.22), custom_call_target="Cholesky" | custom-call | tf_op jit(solution)/shard_map/jit(cholesky)/cholesky | solution.py:14
  911.2 12.0 %while.13 = (s32[]{:T(128)}, f32[512,512]{1,0:T(8,128)}, s32[4,2]{0,1:T(2,128)S(1)}, f32[4,128,128]{2,1,0:T(8,128)S(1)}, s32[]{:T(128)}) while((s32[]{:T(128)}, f32[512,512]{1,0:T(8,128)}, s32[4,2]{0,1:T(2,128)S(1)}, f32[4,128,128]{2,1,0:T(8,128)S(1)}, s32[]{:T(128)}) %tuple.127), condition=%wide.while_cond.clone.2, body=%wide.while_body.clone.2.sunk | while | flops 2 | bytes 131189 | solution.py:16
  923.2 39.3 %custom-call.50 = f32[4,128,128]{1,2,0:T(8,128)S(1)} custom-call(f32[4,128,128]{2,1,0:T(8,128)S(1)} %get-tuple-element.46), custom_call_target="InvertDiagBlocksLowerTriangular" | custom-call | tf_op jit(solution)/shard_map/triangular_solve/custom-call.3 | solution.py:16
  970.3 6.0 fusion.16
  976.3 13.6 %negate_convert_fusion = bf16[1024,1024]{1,0:T(8,128)(2,1)S(1)} fusion(f32[1024,1024]{1,0:T(8,128)S(1)} %copy-done.18, f32[512,512]{1,0:T(8,128)S(1)} %copy-done.7, f32[128,512]{1,0:T(8,128)S(1)} %fusion.113, f32[128,512]{1,0:T(8,128)S(1)} %fusion.114, f32[128,512]{1,0:T(8,128)S(1)} %fusion.116, f32[128,512]{1,0:T(8,128)S(1)} %fusion.77, ...), kind=kOutput, calls=%fused_computation.30 | convolution fusion | flops 12894339072 | bytes 9437184 | tf_op jit(solution)/shard_map/dot_general | solution.py:22
  990.0 26.9 %fusion.13 = bf16[256,2048]{1,0:T(8,128)(2,1)} fusion(bf16[1024,1024]{1,0:T(8,128)(2,1)S(1)} %copy-done.13, bf16[1024,1024]{1,0:T(8,128)(2,1)S(1)} %fusion.16, bf16[1024,1024]{1,0:T(8,128)(2,1)S(1)} %negate_convert_fusion, bf16[2048,2048]{1,0:T(8,128)(2,1)} %get-tuple-element.377, s32[]{:T(128)S(6)} %select_n.31), kind=kOutput, calls=%fused_computation.34 | convolution fusion | flops 2181562368 | bytes 8388612 | tf_op jit(solution)/shard_map/dot_general | solution.py:83
  (263 shorter events, 181.6 us)
Async XLA Ops:
  6.5 4.0 copy-start
  6.5 59.5 %all-gather.3.cloned.1.call-start = ((), (), s32[]{:S(2)}) async-start(), calls=%async_computation | async-start | bytes 9437184 | tf_op jit(solution)/shard_map/all_gather | solution.py:62
  7.3 188.6 %all-reduce.7.cloned.1.call-start = ((), (), s32[]{:S(2)}) async-start(), calls=%async_computation.1 | async-start | bytes 4194304 | tf_op jit(solution)/shard_map/psum | solution.py:78
  91.7 3.5 copy-start.14
  105.3 178.4 %all-gather.5.cloned.1.call-start = ((), (), s32[]{:S(2)}) async-start(), calls=%async_computation.2 | async-start | bytes 18874368 | tf_op jit(solution)/shard_map/all_gather | solution.py:79
  434.1 1.0 copy-start.8
  574.7 3.5 copy-start.15
  575.1 8.2 copy-start.5
  581.4 8.8 copy-start.11
  583.3 35.5 %copy-start.2 = (f32[512,512]{1,0:T(8,128)}, f32[512,512]{1,0:T(8,128)S(1)}, u32[]{:S(2)}) copy-start(f32[512,512]{1,0:T(8,128)S(1)} %convolution_negate_fusion.1) | copy-start | bytes 3145732
  618.8 18.2 %copy-start.16 = (f32[1024,1024]{1,0:T(8,128)}, f32[1024,1024]{1,0:T(8,128)S(1)}, u32[]{:S(2)}) copy-start(f32[1024,1024]{1,0:T(8,128)S(1)} %fusion.9) | copy-start | bytes 12582916
  642.3 1.0 copy-start.10
  793.9 7.3 copy-start.3
  794.0 7.3 copy-start.6
  794.0 7.2 copy-start.12
  794.0 7.2 copy-start.17
  821.1 1.0 copy-start.9
  909.8 58.6 %copy-start.4 = (f32[512,512]{1,0:T(8,128)S(1)}, f32[512,512]{1,0:T(8,128)}, u32[]{:S(2)}) copy-start(f32[512,512]{1,0:T(8,128)} %fusion.170) | copy-start | bytes 3145732
  962.9 7.4 copy-start.7
  968.5 7.9 copy-start.18
  976.3 13.7 %copy-start.13 = (bf16[1024,1024]{1,0:T(8,128)(2,1)S(1)}, bf16[1024,1024]{1,0:T(8,128)(2,1)}, u32[]{:S(2)}) copy-start(bf16[1024,1024]{1,0:T(8,128)(2,1)} %fusion.173) | copy-start | bytes 6291460
  990.0 26.9 %copy-start.1 = (bf16[128,8,128]{2,1,0:T(8,128)(2,1)S(1)}, bf16[128,8,128]{2,1,0:T(8,128)(2,1)}, u32[]{:S(2)}) copy-start(bf16[128,8,128]{2,1,0:T(8,128)(2,1)} %param.10) | copy-start | bytes 786436
Sparse Core Ops, SparseCore 0:
  9.0 57.0 all-gather.2
  105.4 90.4 all-reduce.6
  197.6 86.0 all-gather.4
where the time goes:
time: 1030 us; the launch traced here: 1020 us
  other arithmetic  503 us (49%)
  waiting for transfers between devices  229 us (22%)
  matrix products  182 us (18%)
  local copies, waits for them, and re-layouts  84.3 us (8%)
  between operations  25.2 us (2%)
    another operation x59, other arithmetic, inverse_factor(): lower = jnp.linalg.cholesky(matrix)  317 us
    another operation x11, other arithmetic, inverse_factor(): lax.linalg.triangular_solve(lower, identity, left_side=True, lower=True)  163 us
    psum x1, waiting for transfers between devices, shards(): panel_total = lax.psum(gram_panel + paw, 'grid')  90.3 us
    all_gather x1, waiting for transfers between devices, shards(): metric = lax.all_gather(panel_total, 'band', axis=0, tiled=True)  87.6 us
    all_gather x1, waiting for transfers between devices, shards(): gathered = lax.all_gather(orbitals, 'band', axis=1, tiled=True)  50.7 us
    another operation x53, local copies, waits for them, and re-layouts, inverse_factor(): lax.linalg.triangular_solve(lower, identity, left_side=True, lower=True)  42.3 us
    dot_general x3, matrix products, inverse_factor(): jnp.dot(matrix[half:, :half], upper_inv.T, precision=lax.Precision.HIGHEST)  38 us
    dot_general x1, matrix products, shards(): jnp.dot(mine, inverse.T, preferred_element_type=jnp.float32)  26.9 us
  transfers between devices with their start and end apart: 3, of which 3 were waited for; matrix products, arithmetic and copies ran while one was open for 1% of the time, Pallas kernels for 0%

commit v1 on v0

--- a/solution.py
+++ b/solution.py
@@ -76,7 +76,9 @@
         precision=lax.Precision.HIGHEST,
     )
     panel_total = lax.psum(gram_panel + paw, "grid")
-    metric = lax.all_gather(panel_total, "band", axis=0, tiled=True)
+    metric = jnp.concatenate(
+        lax.all_to_all(jnp.stack([panel_total] * lax.axis_size("band")), "band", 0, 0), axis=0
+    )
     height = orbitals.shape[0] // nbands
     mine = lax.dynamic_slice_in_dim(gathered, band_index * height, height, 0)
     inverse = inverse_factor(metric).astype(jnp.bfloat16)

time: 1030 us -> 1150 us (1.12)
  waiting for transfers between devices: 229 us -> 325 us
  local copies, waits for them, and re-layouts: 84.3 us -> 107 us
    all_to_all x0 -> x1, waiting for transfers between devices: none -> 184 us  [shards(): lax.all_to_all(jnp.stack([panel_total] * lax.axis_size('band')), 'band',...]
    all_gather x1 -> x0, waiting for transfers between devices: 87.6 us -> none  [shards(): metric = lax.all_gather(panel_total, 'band', axis=0, tiled=True)]
where the time goes in v1:
time: 1150 us; the launch traced here: 1140 us
  other arithmetic  503 us (44%)
  waiting for transfers between devices  325 us (28%)
  matrix products  173 us (15%)
  local copies, waits for them, and re-layouts  107 us (9%)
  between operations  25.6 us (2%)
    another operation x59, other arithmetic, inverse_factor(): lower = jnp.linalg.cholesky(matrix)  317 us
    all_to_all x1, waiting for transfers between devices, shards(): lax.all_to_all(jnp.stack([panel_total] * lax.axis_size('band')), 'band',...  184 us
    another operation x11, other arithmetic, inverse_factor(): lax.linalg.triangular_solve(lower, identity, left_side=True, lower=True)  163 us
    psum x1, waiting for transfers between devices, shards(): panel_total = lax.psum(gram_panel + paw, 'grid')  90.6 us
    all_gather x1, waiting for transfers between devices, shards(): gathered = lax.all_gather(orbitals, 'band', axis=1, tiled=True)  50.7 us
    another operation x53, local copies, waits for them, and re-layouts, inverse_factor(): lax.linalg.triangular_solve(lower, identity, left_side=True, lower=True)  43.5 us
    dot_general x3, matrix products, inverse_factor(): jnp.dot(matrix[half:, :half], upper_inv.T, precision=lax.Precision.HIGHEST)  36.9 us
    dot_general x1, matrix products, shards(): jnp.dot(mine, inverse.T, preferred_element_type=jnp.float32)  26.8 us
  transfers between devices with their start and end apart: 3, of which 3 were waited for; matrix products, arithmetic and copies ran while one was open for 1% of the time, Pallas kernels for 0%

profile of v1, /device:TPU:1, one launch (start us, length us, event | category | flops | bytes accessed | tf_op | source)
XLA Modules:
  0.0 1141.9 jit_solution(14004281755383319010)
XLA Ops:
  15.4 50.7 %all-gather.2.cloned.1.call-done = bf16[2048,2048]{1,0:T(8,128)(2,1)} async-done(((bf16[2048,256]{1,0:T(8,128)(2,1)}), bf16[2048,2048]{1,0:T(8,128)(2,1)}) %all-gather.2.cloned.1.call-update) | async-done | bytes 8388624 | tf_op jit(solution)/shard_map/all_gather | solution.py:62
  66.1 25.9 %while.9 = (s32[]{:T(128)}, bf16[2048,2048]{1,0:T(8,128)(2,1)}, s32[8,2]{0,1:T(2,128)S(1)}, bf16[8,128,2048]{2,1,0:T(8,128)(2,1)}, s32[]{:T(128)}) while((s32[]{:T(128)}, bf16[2048,2048]{1,0:T(8,128)(2,1)}, s32[8,2]{0,1:T(2,128)S(1)}, bf16[8,128,2048]{2,1,0:T(8,128)(2,1)}, s32[]{:T(128)}) %tuple.104), condition=%wide.while_cond.1, body=%wide.while_body.1.sunk | while | flops 2 | bytes 1049689 | solution.py:41
  101.0 90.6 %all-reduce.7.cloned.1.call-done = f32[256,2048]{1,0:T(8,128)} async-done(((f32[256,2048]{1,0:T(8,128)}), f32[256,2048]{1,0:T(8,128)}) %all-reduce.7.cloned.1.call-update) | async-done | bytes 2097168 | tf_op jit(solution)/shard_map/psum | solution.py:78
  193.5 7.2 stack.2
  200.7 7.7 all-to-all-start
  208.5 183.5 %all-to-all-done = f32[8,256,2048]{1,2,0:T(8,128)} async-done(((f32[8,256,2048]{1,2,0:T(8,128)}), f32[8,256,2048]{1,2,0:T(8,128)}, u32[]{:S(2)}, u32[]{:S(2)}) %all-to-all-start) | async-done | bytes 16777248 | tf_op jit(solution)/shard_map/all_to_all | solution.py:80
  392.0 7.3 copy.47
  407.0 11.7 %cholesky.462 = f32[128,128]{1,0:T(8,128)S(1)} custom-call(f32[128,128]{1,0:T(8,128)S(1)} %cholesky.746), custom_call_target="Cholesky" | custom-call | tf_op jit(solution)/shard_map/jit(cholesky)/cholesky | solution.py:14
  418.7 9.8 custom-call.35
  429.3 11.7 %cholesky.481 = f32[128,128]{1,0:T(8,128)S(1)} custom-call(f32[128,128]{1,0:T(8,128)S(1)} %cholesky.750), custom_call_target="Cholesky" | custom-call | tf_op jit(solution)/shard_map/jit(cholesky)/cholesky | solution.py:14
  441.1 10.2 custom-call.36
  451.9 11.7 %cholesky.502 = f32[128,128]{1,0:T(8,128)S(1)} custom-call(f32[128,128]{1,0:T(8,128)S(1)} %cholesky.755), custom_call_target="Cholesky" | custom-call | tf_op jit(solution)/shard_map/jit(cholesky)/cholesky | solution.py:14
  464.3 9.8 custom-call.37
  474.7 11.7 %cholesky.519 = f32[128,128]{1,0:T(8,128)S(1)} custom-call(f32[128,128]{1,0:T(8,128)S(1)} %convolution_subtract_fusion.25), custom_call_target="Cholesky" | custom-call | tf_op jit(solution)/shard_map/jit(cholesky)/cholesky | solution.py:14
  490.7 8.1 while.10
  498.8 39.3 %custom-call.38 = f32[4,128,128]{1,2,0:T(8,128)S(1)} custom-call(f32[4,128,128]{2,1,0:T(8,128)S(1)} %get-tuple-element.43), custom_call_target="InvertDiagBlocksLowerTriangular" | custom-call | tf_op jit(solution)/shard_map/triangular_solve/custom-call.3 | solution.py:16
  555.9 12.1 %cholesky.534 = f32[128,128]{1,0:T(8,128)S(1)} custom-call(f32[128,128]{1,0:T(8,128)S(1)} %cholesky.759), custom_call_target="Cholesky" | custom-call | tf_op jit(solution)/shard_map/jit(cholesky)/cholesky | solution.py:14
  568.2 9.8 custom-call.39
  580.5 11.7 %cholesky.553 = f32[128,128]{1,0:T(8,128)S(1)} custom-call(f32[128,128]{1,0:T(8,128)S(1)} %cholesky.763), custom_call_target="Cholesky" | custom-call | tf_op jit(solution)/shard_map/jit(cholesky)/cholesky | solution.py:14
  593.7 9.8 custom-call.40
  605.1 11.9 %cholesky.574 = f32[128,128]{1,0:T(8,128)S(1)} custom-call(f32[128,128]{1,0:T(8,128)S(1)} %cholesky.768), custom_call_target="Cholesky" | custom-call | tf_op jit(solution)/shard_map/jit(cholesky)/cholesky | solution.py:14
  617.7 9.8 custom-call.41
  628.9 11.7 %cholesky.591 = f32[128,128]{1,0:T(8,128)S(1)} custom-call(f32[128,128]{1,0:T(8,128)S(1)} %convolution_subtract_fusion.24), custom_call_target="Cholesky" | custom-call | tf_op jit(solution)/shard_map/jit(cholesky)/cholesky | solution.py:14
  645.1 12.0 %while.11 = (s32[]{:T(128)}, f32[512,512]{1,0:T(8,128)}, s32[4,2]{0,1:T(2,128)S(1)}, f32[4,128,128]{2,1,0:T(8,128)S(1)}, s32[]{:T(128)}) while((s32[]{:T(128)}, f32[512,512]{1,0:T(8,128)}, s32[4,2]{0,1:T(2,128)S(1)}, f32[4,128,128]{2,1,0:T(8,128)S(1)}, s32[]{:T(128)}) %tuple.123), condition=%wide.while_cond.clone, body=%wide.while_body.clone.sunk | while | flops 2 | bytes 131181 | solution.py:16
  657.1 39.3 %custom-call.42 = f32[4,128,128]{1,2,0:T(8,128)S(1)} custom-call(f32[4,128,128]{2,1,0:T(8,128)S(1)} %get-tuple-element.44), custom_call_target="InvertDiagBlocksLowerTriangular" | custom-call | tf_op jit(solution)/shard_map/triangular_solve/custom-call.3 | solution.py:16
  705.1 28.6 %fusion.9 = f32[1024,1024]{1,0:T(8,128)S(1)} fusion(f32[2048,2048]{0,1:T(8,128)} %bitcast.228, f32[512,512]{1,0:T(8,128)S(1)} %copy-done.8, f32[128,512]{1,0:T(8,128)S(1)} %fusion.125, f32[128,512]{1,0:T(8,128)S(1)} %fusion.126, f32[128,512]{1,0:T(8,128)S(1)} %fusion.128, f32[128,512]{1,0:T(8,128)S(1)} %fusion.81, f32[512,512]{1,0:T(8,128)S(1)} %convolution_negate_fusion.1), kind=kOutput, calls=%fused_computation.24 | convolution fusion | flops 12892241920 | bytes 11534336 | tf_op jit(solution)/shard_map/dot_general | solution.py:19
  733.8 16.8 %fusion.172 = f32[1024,1024]{1,0:T(8,128)} fusion(f32[1024,1024]{1,0:T(8,128)S(1)} %fusion.9, f32[512,512]{1,0:T(8,128)S(1)} %copy-done.8, f32[128,512]{1,0:T(8,128)S(1)} %fusion.125, f32[128,512]{1,0:T(8,128)S(1)} %fusion.126, f32[128,512]{1,0:T(8,128)S(1)} %fusion.128, f32[128,512]{1,0:T(8,128)S(1)} %fusion.81, f32[512,512]{1,0:T(8,128)S(1)} %convolution_negate_fusion.1), kind=kOutput, calls=%fused_computation.324 | convolution fusion | flops 12892241920 | bytes 11534336 | tf_op jit(solution)/shard_map/dot_general | solution.py:24
  750.5 16.0 %slice_subtract_fusion = f32[1024,1024]{0,1:T(8,128)S(1)} fusion(f32[2048,2048]{0,1:T(8,128)} %bitcast.229, f32[1024,1024]{1,0:T(8,128)S(1)} %fusion.9), kind=kOutput, calls=%fused_computation.26 | convolution fusion | flops 12885950464 | bytes 16777216 | tf_op jit(solution)/shard_map/dot_general | solution.py:20
  773.6 11.7 %cholesky.606 = f32[128,128]{1,0:T(8,128)S(1)} custom-call(f32[128,128]{1,0:T(8,128)S(1)} %cholesky.772), custom_call_target="Cholesky" | custom-call | tf_op jit(solution)/shard_map/jit(cholesky)/cholesky | solution.py:14
  785.5 9.8 custom-call.43
  797.8 11.7 %cholesky.625 = f32[128,128]{1,0:T(8,128)S(1)} custom-call(f32[128,128]{1,0:T(8,128)S(1)} %cholesky.776), custom_call_target="Cholesky" | custom-call | tf_op jit(solution)/shard_map/jit(cholesky)/cholesky | solution.py:14
  810.9 10.0 custom-call.44
  822.5 11.7 %cholesky.646 = f32[128,128]{1,0:T(8,128)S(1)} custom-call(f32[128,128]{1,0:T(8,128)S(1)} %cholesky.781), custom_call_target="Cholesky" | custom-call | tf_op jit(solution)/shard_map/jit(cholesky)/cholesky | solution.py:14
  834.9 9.8 custom-call.45
  846.2 11.7 %cholesky.663 = f32[128,128]{1,0:T(8,128)S(1)} custom-call(f32[128,128]{1,0:T(8,128)S(1)} %convolution_subtract_fusion.23), custom_call_target="Cholesky" | custom-call | tf_op jit(solution)/shard_map/jit(cholesky)/cholesky | solution.py:14
  862.8 11.8 %while.12 = (s32[]{:T(128)}, f32[512,512]{1,0:T(8,128)}, s32[4,2]{0,1:T(2,128)S(1)}, f32[4,128,128]{2,1,0:T(8,128)S(1)}, s32[]{:T(128)}) while((s32[]{:T(128)}, f32[512,512]{1,0:T(8,128)}, s32[4,2]{0,1:T(2,128)S(1)}, f32[4,128,128]{2,1,0:T(8,128)S(1)}, s32[]{:T(128)}) %tuple.124), condition=%wide.while_cond.clone.1, body=%wide.while_body.clone.1.sunk | while | flops 2 | bytes 131181 | solution.py:16
  874.7 39.3 %custom-call.46 = f32[4,128,128]{1,2,0:T(8,128)S(1)} custom-call(f32[4,128,128]{2,1,0:T(8,128)S(1)} %get-tuple-element.45), custom_call_target="InvertDiagBlocksLowerTriangular" | custom-call | tf_op jit(solution)/shard_map/triangular_solve/custom-call.3 | solution.py:16
  940.3 11.7 %cholesky.678 = f32[128,128]{1,0:T(8,128)S(1)} custom-call(f32[128,128]{1,0:T(8,128)S(1)} %cholesky.785), custom_call_target="Cholesky" | custom-call | tf_op jit(solution)/shard_map/jit(cholesky)/cholesky | solution.py:14
  952.2 9.8 custom-call.47
  964.6 11.7 %cholesky.697 = f32[128,128]{1,0:T(8,128)S(1)} custom-call(f32[128,128]{1,0:T(8,128)S(1)} %cholesky.789), custom_call_target="Cholesky" | custom-call | tf_op jit(solution)/shard_map/jit(cholesky)/cholesky | solution.py:14
  977.7 10.2 custom-call.48
  989.4 11.7 %cholesky.718 = f32[128,128]{1,0:T(8,128)S(1)} custom-call(f32[128,128]{1,0:T(8,128)S(1)} %cholesky.794), custom_call_target="Cholesky" | custom-call | tf_op jit(solution)/shard_map/jit(cholesky)/cholesky | solution.py:14
  1001.9 9.8 custom-call.49
  1013.1 11.7 %cholesky.735 = f32[128,128]{1,0:T(8,128)S(1)} custom-call(f32[128,128]{1,0:T(8,128)S(1)} %convolution_subtract_fusion.22), custom_call_target="Cholesky" | custom-call | tf_op jit(solution)/shard_map/jit(cholesky)/cholesky | solution.py:14
  1029.4 11.8 %while.13 = (s32[]{:T(128)}, f32[512,512]{1,0:T(8,128)}, s32[4,2]{0,1:T(2,128)S(1)}, f32[4,128,128]{2,1,0:T(8,128)S(1)}, s32[]{:T(128)}) while((s32[]{:T(128)}, f32[512,512]{1,0:T(8,128)}, s32[4,2]{0,1:T(2,128)S(1)}, f32[4,128,128]{2,1,0:T(8,128)S(1)}, s32[]{:T(128)}) %tuple.125), condition=%wide.while_cond.clone.2, body=%wide.while_body.clone.2.sunk | while | flops 2 | bytes 131181 | solution.py:16
  1041.2 39.3 %custom-call.50 = f32[4,128,128]{1,2,0:T(8,128)S(1)} custom-call(f32[4,128,128]{2,1,0:T(8,128)S(1)} %get-tuple-element.46), custom_call_target="InvertDiagBlocksLowerTriangular" | custom-call | tf_op jit(solution)/shard_map/triangular_solve/custom-call.3 | solution.py:16
  1094.3 13.6 %negate_convert_fusion = bf16[1024,1024]{1,0:T(8,128)(2,1)S(1)} fusion(f32[1024,1024]{1,0:T(8,128)S(1)} %copy-done.20, f32[512,512]{1,0:T(8,128)S(1)} %copy-done.10, f32[128,512]{1,0:T(8,128)S(1)} %fusion.113, f32[128,512]{1,0:T(8,128)S(1)} %fusion.114, f32[128,512]{1,0:T(8,128)S(1)} %fusion.116, f32[128,512]{1,0:T(8,128)S(1)} %fusion.77, ...), kind=kOutput, calls=%fused_computation.30 | convolution fusion | flops 12894339072 | bytes 9437184 | tf_op jit(solution)/shard_map/dot_general | solution.py:22
  1107.9 26.8 %fusion.13 = bf16[256,2048]{1,0:T(8,128)(2,1)} fusion(bf16[1024,1024]{1,0:T(8,128)(2,1)S(1)} %copy-done.18, bf16[1024,1024]{1,0:T(8,128)(2,1)S(1)} %fusion.16, bf16[1024,1024]{1,0:T(8,128)(2,1)S(1)} %negate_convert_fusion, bf16[2048,2048]{1,0:T(8,128)(2,1)} %get-tuple-element.366, s32[]{:T(128)S(6)} %select_n.31), kind=kOutput, calls=%fused_computation.34 | convolution fusion | flops 2181562368 | bytes 8388612 | tf_op jit(solution)/shard_map/dot_general | solution.py:85
  (269 shorter events, 203.3 us)
Async XLA Ops:
  6.5 5.3 copy-start
  6.5 59.5 %all-gather.2.cloned.1.call-start = ((), (), s32[]{:S(2)}) async-start(), calls=%async_computation.1 | async-start | bytes 9437184 | tf_op jit(solution)/shard_map/all_gather | solution.py:62
  7.3 184.4 %all-reduce.7.cloned.1.call-start = ((), (), s32[]{:S(2)}) async-start(), calls=%async_computation.2 | async-start | bytes 4194304 | tf_op jit(solution)/shard_map/psum | solution.py:78
  91.9 5.4 copy-start.2
  94.9 2.5 copy-start.4
  200.7 191.3 %all-to-all-start = ((f32[8,256,2048]{1,2,0:T(8,128)}), f32[8,256,2048]{1,2,0:T(8,128)}, u32[]{:S(2)}, u32[]{:S(2)}) async-start(f32[8,256,2048]{1,2,0:T(8,128)} %stack.2), calls=%async_computation | async-start | bytes 33554432 | tf_op jit(solution)/shard_map/all_to_all | solution.py:80
  399.4 5.7 copy-start.3
  554.9 1.0 copy-start.13
  696.4 3.5 copy-start.19
  696.9 8.2 copy-start.8
  703.2 30.5 %copy-start.16 = (f32[128,512]{1,0:T(8,128)}, f32[128,512]{1,0:T(8,128)S(1)}, u32[]{:S(2)}) copy-start(f32[128,512]{1,0:T(8,128)S(1)} %fusion.125) | copy-start | bytes 786436
  705.1 28.7 %copy-start.5 = (f32[512,512]{1,0:T(8,128)}, f32[512,512]{1,0:T(8,128)S(1)}, u32[]{:S(2)}) copy-start(f32[512,512]{1,0:T(8,128)S(1)} %convolution_negate_fusion.1) | copy-start | bytes 3145732
  766.6 2.0 copy-start.11
  772.6 1.0 copy-start.15
  914.0 7.1 copy-start.12
  924.6 4.8 copy-start.6
  924.6 4.8 copy-start.9
  924.7 4.8 copy-start.17
  939.4 1.0 copy-start.14
  1028.1 58.3 %copy-start.7 = (f32[512,512]{1,0:T(8,128)S(1)}, f32[512,512]{1,0:T(8,128)}, u32[]{:S(2)}) copy-start(f32[512,512]{1,0:T(8,128)} %fusion.170) | copy-start | bytes 3145732
  1080.9 7.4 copy-start.10
  1086.4 7.9 copy-start.20
  1094.3 13.6 %copy-start.18 = (bf16[1024,1024]{1,0:T(8,128)(2,1)S(1)}, bf16[1024,1024]{1,0:T(8,128)(2,1)}, u32[]{:S(2)}) copy-start(bf16[1024,1024]{1,0:T(8,128)(2,1)} %fusion.173) | copy-start | bytes 6291460
  1107.9 26.8 %copy-start.1 = (bf16[128,8,128]{2,1,0:T(8,128)(2,1)S(1)}, bf16[128,8,128]{2,1,0:T(8,128)(2,1)}, u32[]{:S(2)}) copy-start(bf16[128,8,128]{2,1,0:T(8,128)(2,1)} %param.10) | copy-start | bytes 786436
Sparse Core Ops, SparseCore 0:
  9.0 57.0 all-gather.1
  101.2 90.4 all-reduce.6
